TPU v7x, 512 devices: a 8x2x16 block of a 8x8x16 slice. The times are simulated.
512 devices in a mesh: grp: 2 (over y), ep: 128 (over x, z), tp: 2 (over core).
Axes of the slice: x: 8, y: 2, z: 16, core: 2. Of those that a mesh axis runs over, the one named last changes fastest.
The devices are a block of a 8x8x16 slice.
Arguments:
- queries: bfloat16 [16384, 16, 576], P(('grp', 'ep'), 'tp'), parts along dimension 0, may hold values from -450 to 450
- latent_cache: bfloat16 [768, 512, 576], P(('grp', 'ep'), 'tp'), parts along dimension 0, may hold values from -6 to 6
- residual: bfloat16 [16384, 2048], P(('grp', 'ep')), parts along dimension 0, may hold values from -8 to 8
- token_request: int32 [16384], P(('grp', 'ep')), parts along dimension 0, may hold values from 0 to 2, as said below
- token_visible: int32 [16384], P(('grp', 'ep')), parts along dimension 0, may hold values from 1 to 512, as said below
- value_proj: bfloat16 [16, 512, 128], P('tp', 'ep'), may hold values from -0.25 to 0.25
- out_proj: bfloat16 [2048, 2048], P('tp', 'ep'), may hold values from -0.125 to 0.125
- norm_gain: float32 [2048], replicated, may hold values from 0.1 to 1.9
- router: bfloat16 [2048, 64], replicated, may hold values from -0.0390625 to 0.0390625
- expert_ids: int32 [16384, 6], P(('grp', 'ep')), parts along dimension 0, may hold values from 0 to 63, all different within a row; in each aligned block of 64 rows (0 to 63, 64 to 127, ...) at most 8 rows name the same one
- gate_weight: bfloat16 [128, 2048, 384], P('ep', None, 'tp'), may hold values from -0.125 to 0.125
- up_weight: bfloat16 [128, 2048, 384], P('ep', None, 'tp'), may hold values from -0.125 to 0.125
- down_weight: bfloat16 [128, 384, 2048], P('ep', 'tp'), may hold values from -0.21875 to 0.21875
Outputs:
- hidden: bfloat16 [16384, 2048], P(('grp', 'ep'), 'tp'), parts along dimension 0
- expert_out: bfloat16 [16384, 2048], P(('grp', 'ep'), 'tp'), parts along dimension 0
There are 2 independent parts, one for each index of `grp`. A program takes and returns all parts, laid end to end along the dimension named above; an argument that names none is the same for every part. Nothing has to cross between parts.
Inputs may be any that keep to these rules, and one draw needn't show every extreme that they name: `token_request`: in each ep block, 62 tokens belong to request 0, a prefill span, and each other request has exactly one token; the tokens' order in the block is arbitrary. `token_visible`: the span's tokens read consecutive counts s + 1 to s + 62; 512 is reached in every draw. `expert_ids`: each row names 6 different experts; among the 64 tokens of one ep index no expert is named by more than 8 tokens, and this bound is reached.
All inputs are finite; a program needn't handle non-finite values.
Results may differ from a plain program's by a relative error of at most 0.018.
Values may be sent and summed in bfloat16 or wider, within the bound.
A program may use at most 64 MiB of HBM per device.

v0:
```python
import jax
import jax.numpy as jnp
from jax import lax
from jax.sharding import Mesh
from jax.sharding import PartitionSpec as P

LATENT = 512
VDIM = 128
EXPERTS = 64
TOPK = 6
GROUPS = 2
CAP = 8
PIECES = 128
EP = ("ep_0", "ep_1")
GRP_EP = ("grp", "ep_0", "ep_1")
score_scale = 192.0 ** (-0.5)
epsilon = 1e-06


def from_everyone(value, axis):
    peers = lax.axis_size(axis)
    return lax.all_to_all(
        jnp.broadcast_to(value[None], (peers, *value.shape)), axis, 0, 0, tiled=True
    )


def laid_out(pieces, dim):
    lengths = list(pieces.shape[1:])
    lengths[dim] *= pieces.shape[0]
    return jnp.moveaxis(pieces, 0, dim).reshape(lengths)


def collect(value, axis, dim):
    pieces = from_everyone(value, axis)
    return laid_out(pieces, dim)


def of_everyone(value, axis):
    return from_everyone(value, axis).max(axis=0)


def split_up(value, dim, peers):
    before, after = (value.shape[:dim], value.shape[dim + 1 :])
    return jnp.moveaxis(value.reshape(*before, peers, -1, *after), dim, 0)


def sent_and_summed(value, axis, dim):
    peers = lax.axis_size(axis)
    pieces = lax.all_to_all(split_up(value, dim, peers), axis, 0, 0, tiled=True)
    return jnp.sum(pieces, axis=0)


def sent_together(arrays, axis, dim, along):
    columns = [a.reshape(*a.shape[:along], -1) for a in arrays]
    both = jnp.concatenate(columns, axis=along)
    result, at, outs = (sent_and_summed(both, axis, dim), 0, [])
    for a, column in zip(arrays, columns):
        piece = result[..., at : at + column.shape[along]]
        outs.append(piece.reshape(*piece.shape[:along], *a.shape[along:]))
        at += column.shape[along]
    return tuple(outs)


def stacked_from(value, axes, order):
    pieces = value[None]
    for k in order:
        pieces = lax.all_gather(pieces, axes[k], axis=0, tiled=True)
    carried = [lax.axis_size(axes[k]) for k in reversed(order)]
    pieces = pieces.reshape(*carried, *value.shape)
    turned = sorted(range(len(order)), key=lambda place: order[len(order) - 1 - place])
    return pieces.transpose(*turned, *range(len(order), pieces.ndim)).reshape(-1, *value.shape)


def whole_of(value, axes, order, dim):
    return laid_out(stacked_from(value, axes, order), dim)


def over_copies(value, axis):
    everything = from_everyone(value, axis)
    return jnp.sum(everything, axis=0)


def masked_scores(queries, block_rows, token_request, token_visible, offset):
    per_request = block_rows.shape[1]
    flat_rows = block_rows.reshape(-1, block_rows.shape[2])
    scores = (
        jnp.einsum("thc,kc->thk", queries, flat_rows, preferred_element_type=jnp.float32)
        * score_scale
    )
    column = jnp.arange(flat_rows.shape[0], dtype=jnp.int32)
    owner_id = column // per_request
    position = column % per_request + offset
    allowed = (owner_id[None, :] == token_request[:, None]) & (
        position[None, :] < token_visible[:, None]
    )
    return (jnp.where(allowed[:, None, :], scores, -jnp.inf), flat_rows)


def weighted_rows(scores, row_peak, flat_rows):
    weights = jnp.exp(scores - row_peak[:, :, None]).astype(jnp.bfloat16)
    totals = jnp.sum(weights.astype(jnp.float32), axis=2)
    summed = jnp.einsum(
        "thk,kc->thc", weights, flat_rows[:, :LATENT], preferred_element_type=jnp.float32
    )
    return (summed, totals)


def expert_block(arrived, gate_weight, up_weight, down_weight):
    gate_vals = jnp.einsum("prd,pdf->prf", arrived, gate_weight, preferred_element_type=jnp.float32)
    up_vals = jnp.einsum("prd,pdf->prf", arrived, up_weight, preferred_element_type=jnp.float32)
    activated = (jax.nn.silu(gate_vals) * up_vals).astype(jnp.bfloat16)
    return jnp.einsum(
        "prf,pfd->prd", activated, down_weight, preferred_element_type=jnp.float32
    ).astype(jnp.bfloat16)


def body(
    queries,
    latent_cache,
    residual,
    token_request,
    token_visible,
    value_proj,
    out_proj,
    norm_gain,
    router,
    expert_ids,
    gate_weight,
    up_weight,
    down_weight,
):
    all_heads = collect(queries, "tp", 1)
    offset = lax.axis_index("tp") * latent_cache.shape[1]
    scores, flat_rows = masked_scores(all_heads, latent_cache, token_request, token_visible, offset)
    row_peak = of_everyone(jnp.max(scores, axis=2), "tp")
    part_sum, part_total = weighted_rows(scores, row_peak, flat_rows)
    summed, totals = sent_together((part_sum, part_total), "tp", 1, 2)
    context = (summed / totals[:, :, None]).astype(jnp.bfloat16)
    tokens_here = context.shape[0]
    heads_here = context.shape[1]
    head_values = jnp.einsum(
        "thl,hlv->thv",
        context,
        whole_of(value_proj, EP, (0, 1), 1),
        preferred_element_type=jnp.float32,
    )
    heads_out = head_values.astype(jnp.bfloat16).reshape(tokens_here, heads_here * VDIM)
    attention_part = jnp.dot(
        heads_out, whole_of(out_proj, EP, (0, 1), 1), preferred_element_type=jnp.float32
    )
    attention = over_copies(attention_part, "tp")
    hidden = (residual.astype(jnp.float32) + attention).astype(jnp.bfloat16)
    hidden_wide = hidden.astype(jnp.float32)
    normed = (
        hidden_wide
        * lax.rsqrt(jnp.mean(hidden_wide * hidden_wide, axis=1, keepdims=True) + epsilon)
        * norm_gain
    ).astype(jnp.bfloat16)
    logits = jnp.dot(normed, router, preferred_element_type=jnp.float32)
    gate_share = jax.nn.softmax(jnp.take_along_axis(logits, expert_ids, axis=1), axis=1).astype(
        jnp.bfloat16
    )
    flat_ids = expert_ids.reshape(-1)
    position_id = jnp.arange(flat_ids.shape[0], dtype=jnp.int32)
    earlier = (flat_ids[:, None] == flat_ids[None, :]) & (
        position_id[None, :] < position_id[:, None]
    )
    slot_ids = (flat_ids * CAP + jnp.sum(earlier.astype(jnp.int32), axis=1)).reshape(
        tokens_here, TOPK
    )
    targets = jnp.arange(EXPERTS * CAP, dtype=jnp.int32)
    matches = slot_ids[:, :, None] == targets[None, None, :]
    picker = jnp.any(matches, axis=1).T.astype(jnp.bfloat16)
    model_width = normed.shape[1]
    mixing = jnp.sum(
        jnp.where(matches, gate_share[:, :, None], jnp.zeros((), jnp.bfloat16)), axis=1
    )
    mixing = jnp.broadcast_to(
        mixing.reshape(tokens_here, EXPERTS, 1, CAP), (tokens_here, EXPERTS, GROUPS, CAP)
    ).reshape(tokens_here, PIECES * CAP)
    core_count = lax.axis_size("tp")
    half_width = model_width // core_count
    core_start = lax.axis_index("tp") * half_width
    normed_share = lax.dynamic_slice_in_dim(normed, core_start, half_width, 1)
    outgoing = jnp.dot(picker, normed_share, preferred_element_type=jnp.float32).astype(
        jnp.bfloat16
    )
    outgoing = jnp.broadcast_to(
        outgoing.reshape(EXPERTS, 1, CAP, half_width), (EXPERTS, GROUPS, CAP, half_width)
    ).reshape(PIECES, CAP, half_width)
    arrived_share = lax.all_to_all(outgoing, EP, split_axis=0, concat_axis=1, tiled=True)
    arrived = lax.all_gather(arrived_share, "tp", axis=2, tiled=True)
    partial_out = expert_block(arrived, gate_weight, up_weight, down_weight)
    swapped = lax.all_to_all(partial_out[None], "tp", split_axis=3, concat_axis=0, tiled=True)
    returned = lax.all_to_all(swapped, EP, split_axis=2, concat_axis=1, tiled=True)
    returned = returned.reshape(core_count, PIECES * CAP, half_width)
    routed = jnp.einsum("tk,qkd->td", mixing, returned, preferred_element_type=jnp.float32)
    expert_out = routed.astype(jnp.bfloat16)
    hidden_part = lax.dynamic_slice_in_dim(hidden, core_start, half_width, 1)
    return (hidden_part, expert_out)


def solution(mesh):
    finer = Mesh(
        mesh.devices.reshape(mesh.shape["grp"], 8, 16, mesh.shape["tp"]),
        ("grp", "ep_0", "ep_1", "tp"),
    )
    in_specs = (
        P(GRP_EP, "tp", None),
        P(GRP_EP, "tp", None),
        P(GRP_EP, None),
        P(GRP_EP),
        P(GRP_EP),
        P("tp", EP, None),
        P("tp", EP),
        P(),
        P(),
        P(GRP_EP, None),
        P(EP, None, "tp"),
        P(EP, None, "tp"),
        P(EP, "tp", None),
    )
    out_specs = (P(GRP_EP, "tp"), P(GRP_EP, "tp"))
    return jax.shard_map(body, mesh=finer, in_specs=in_specs, out_specs=out_specs, check_vma=False)
```

profile of v0, /device:TPU:320, one launch (start us, length us, event | category | flops | bytes accessed | tf_op | source)
XLA Modules:
  0.0 692.1 jit_solution(127817837888464356)
XLA Ops:
  7.3 26.9 %all-gather = bf16[64,4,128]{2,1,0:T(4,128)(2,1)S(1)} all-gather(bf16[8,4,128]{2,1,0:T(4,128)(2,1)} %param.18), channel_id=2, replica_groups=mesh['grp'=2,'ep_0'=8,'ep_1'=16,'tp'=2] {'ep_0'}, dimensions={0}, use_global_device_ids=true | all-gather | bytes 73728 | tf_op jit(solution)/shard_map/all_gather | solution.py:67
  34.9 25.1 %all-gather.1 = bf16[8192,16]{0,1:T(8,128)(2,1)S(1)} all-gather(bf16[1024,16]{0,1:T(8,128)(2,1)} %param.19), channel_id=3, replica_groups=mesh['grp'=2,'ep_0'=8,'ep_1'=16,'tp'=2] {'ep_0'}, dimensions={0}, use_global_device_ids=true | all-gather | bytes 294912 | tf_op jit(solution)/shard_map/all_gather | solution.py:67
  63.2 3.7 all-to-all-start
  69.1 3.2 fusion.4
  72.5 3.7 all_to_all.59
  85.6 4.0 all-to-all-start.2
  97.2 36.4 %all-gather.6.cloned.1.call-done = bf16[128,8,4,128]{3,1,2,0:T(8,128)(2,1)} async-done(((bf16[8,8,4,128]{3,1,2,0:T(8,128)(2,1)}), bf16[128,8,4,128]{3,1,2,0:T(8,128)(2,1)}) %all-gather.6.cloned.1.call-update) | async-done | bytes 1048592 | tf_op jit(solution)/shard_map/all_gather | solution.py:67
  135.8 76.6 %all-gather.8.cloned.1.call-done = bf16[128,1024,16]{1,0,2:T(8,128)(2,1)} async-done(((bf16[8,1024,16]{1,0,2:T(8,128)(2,1)}), bf16[128,1024,16]{1,0,2:T(8,128)(2,1)}) %all-gather.8.cloned.1.call-update) | async-done | bytes 4194320 | tf_op jit(solution)/shard_map/all_gather | solution.py:67
  212.5 4.5 copy.188
  218.5 4.6 all_to_all.60
  224.3 118.1 %all_to_all.61 = bf16[128,8,1024]{2,1,0:T(8,128)(2,1)} all-to-all(bf16[128,8,1024]{2,1,0:T(8,128)(2,1)S(1)} %bitcast.107), channel_id=1, replica_groups=mesh['grp'=2,'ep_0'=8,'ep_1'=16,'tp'=2] {'ep_0','ep_1'}, dimensions={0} | all-to-all | bytes 4194304 | tf_op jit(solution)/shard_map/all_to_all | solution.py:191
  342.5 14.4 %all-gather.10.cloned.1.call-done = bf16[1,1024,2048]{2,1,0:T(8,128)(2,1)} async-done(((bf16[1,1024,1024]{2,1,0:T(8,128)(2,1)}), bf16[1,1024,2048]{2,1,0:T(8,128)(2,1)}) %all-gather.10.cloned.1.call-update) | async-done | bytes 4194320 | tf_op jit(solution)/shard_map/all_gather | solution.py:192
  356.9 4.6 fusion.2
  361.5 7.3 %convert_bitcast_fusion = bf16[1,1,1024,2048]{3,2,1,0:T(8,128)(2,1)} fusion(bf16[1,192,2048]{2,1,0:T(8,128)(2,1)S(1)} %copy-done, bf16[1,1024,2048]{2,1,0:T(8,128)(2,1)} %all-gather.10.cloned.1.call-done, bf16[1,2048,192]{1,2,0:T(8,128)(2,1)} %param.24, f32[1024,192]{0,1:T(8,128)} %fusion.2), kind=kOutput, calls=%fused_computation.6 | convolution fusion | flops 1613889536 | bytes 10747904 | tf_op jit(solution)/shard_map/prf,pfd->prd/dot_general | solution.py:112
  368.8 20.6 %copy.194 = bf16[1,1,1024,2048]{2,1,0,3:T(2,128)(2,1)} copy(bf16[1,1,1024,2048]{3,2,1,0:T(8,128)(2,1)} %convert_bitcast_fusion) | data formatting | bytes 8388608 | tf_op jit(solution)/shard_map/broadcast_in_dim | solution.py:194
  389.9 26.0 %reduce.4 = bf16[2048,1024]{1,0:T(8,128)(2,1)} reduce(bf16[2048,1,1,1024]{3,2,1,0:T(2,128)(2,1)} %bitcast.102, bf16[]{:T(256)} %broadcast.147), dimensions={1,2}, to_apply=%bitcast.85.reduce_sub_computation | reduce | bytes 8388610
  415.9 5.9 reshape.241
  421.8 11.9 %all_to_all.62 = bf16[2,2,524288]{2,1,0:T(2,128)(2,1)} all-to-all(bf16[2,2,524288]{2,1,0:T(2,128)(2,1)} %reshape.241), channel_id=1, replica_groups=mesh['grp'=2,'ep_0'=8,'ep_1'=16,'tp'=2] {'tp'}, dimensions={0} | all-to-all | bytes 8388608 | tf_op jit(solution)/shard_map/all_to_all | solution.py:194
  433.7 7.1 %reshape.242 = bf16[2048,1,1,1024]{3,2,1,0:T(2,128)(2,1)} reshape(bf16[2,2,524288]{2,1,0:T(2,128)(2,1)} %all_to_all.62) | data formatting | bytes 8388608
  440.8 7.1 %copy.200 = bf16[1,1,1024,2048]{2,3,0,1:T(8,128)(2,1)} copy(bf16[1,1,1024,2048]{2,1,0,3:T(2,128)(2,1)} %bitcast.103) | data formatting | bytes 8388608
  447.8 11.3 %copy.195 = bf16[2,1,1024,1024]{3,0,1,2:T(2,128)(2,1)} copy(bf16[2,1,1024,1024]{2,3,0,1:T(8,128)(2,1)} %bitcast.104) | data formatting | bytes 8388608 | tf_op jit(solution)/shard_map/all_to_all | solution.py:194
  459.1 21.4 %all-to-all-start.6 = ((bf16[2,1,1024,1024]{3,0,1,2:T(2,128)(2,1)}), bf16[2,1,1024,1024]{3,0,1,2:T(2,128)(2,1)}, u32[]{:S(2)}, u32[]{:S(2)}) async-start(bf16[2,1,1024,1024]{3,0,1,2:T(2,128)(2,1)} %copy.195), calls=%async_computation.6 | async-start | bytes 8388608 | tf_op jit(solution)/shard_map/all_to_all | solution.py:195
  485.2 186.6 %all-to-all-done.6 = bf16[2,1,1024,1024]{3,0,1,2:T(2,128)(2,1)} async-done(((bf16[2,1,1024,1024]{3,0,1,2:T(2,128)(2,1)}), bf16[2,1,1024,1024]{3,0,1,2:T(2,128)(2,1)}, u32[]{:S(2)}, u32[]{:S(2)}) %all-to-all-start.6) | async-done | bytes 4194336 | tf_op jit(solution)/shard_map/all_to_all | solution.py:195
  671.8 12.4 %convert_reduce_fusion = bf16[1024,1024]{1,0:T(8,128)(2,1)S(1)} fusion(bf16[2,1,1024,1024]{3,0,1,2:T(2,128)(2,1)} %all-to-all-done.6), kind=kLoop, calls=%fused_computation.1 | loop fusion | flops 3145728 | bytes 6291456 | tf_op jit(solution)/shard_map/tk,qkd->td/reduce_sum | solution.py:197
  (82 shorter events, 34.6 us)
Async XLA Ops:
  7.2 354.3 %copy-start = (bf16[1,192,2048]{2,1,0:T(8,128)(2,1)S(1)}, bf16[1,192,2048]{2,1,0:T(8,128)(2,1)}, u32[]{:S(2)}) copy-start(bf16[1,192,2048]{2,1,0:T(8,128)(2,1)} %param.25) | copy-start | bytes 2359300
  7.2 126.4 %all-gather.6.cloned.1.call-start = ((), (), s32[]{:S(2)}) async-start(), calls=%async_computation.7 | async-start | bytes 1114112 | tf_op jit(solution)/shard_map/all_gather | solution.py:67
  34.8 177.6 %all-gather.8.cloned.1.call-start = ((), (), s32[]{:S(2)}) async-start(), calls=%async_computation.8 | async-start | bytes 4456448 | tf_op jit(solution)/shard_map/all_gather | solution.py:67
  60.9 7.5 %copy-start.6 = (s32[64]{0:T(128)S(1)}, s32[64]{0:T(128)}, u32[]{:S(2)}) copy-start(s32[64]{0:T(128)} %param.17) | copy-start | bytes 772
  60.9 7.5 %copy-start.7 = (s32[64]{0:T(128)S(1)}, s32[64]{0:T(128)}, u32[]{:S(2)}) copy-start(s32[64]{0:T(128)} %param.16) | copy-start | bytes 772
  63.2 5.9 all-to-all-start
  85.6 4.4 copy-start.4
  85.6 7.2 %all-to-all-start.2 = ((f32[2,64,8,513]{3,2,1,0:T(8,128)}), f32[2,64,8,513]{3,2,1,0:T(8,128)S(1)}, u32[]{:S(2)}, u32[]{:S(2)}) async-start(f32[2,64,8,513]{3,2,1,0:T(8,128)} %maximum_bitcast_fusion), calls=%async_computation.2 | async-start | bytes 5242880 | tf_op jit(solution)/shard_map/all_to_all | solution.py:49
  89.7 267.2 %all-gather.10.cloned.1.call-start = ((), (), s32[]{:S(2)}) async-start(), calls=%async_computation.9 | async-start | bytes 6291456 | tf_op jit(solution)/shard_map/all_gather | solution.py:192
  218.4 4.8 copy-start.3
  218.4 5.0 copy-start.5
  224.3 132.6 %copy-start.8 = (bf16[1,2048,192]{1,2,0:T(8,128)(2,1)S(1)}, bf16[1,2048,192]{1,2,0:T(8,128)(2,1)}, u32[]{:S(2)}) copy-start(bf16[1,2048,192]{1,2,0:T(8,128)(2,1)} %param.23) | copy-start | bytes 2359300
  459.1 21.7 %copy-start.2 = (bf16[2048,64]{0,1:T(8,128)(2,1)S(1)}, bf16[2048,64]{0,1:T(8,128)(2,1)}, u32[]{:S(2)}) copy-start(bf16[2048,64]{0,1:T(8,128)(2,1)} %param.21) | copy-start | bytes 786436
  459.1 212.7 %all-to-all-start.6 = ((bf16[2,1,1024,1024]{3,0,1,2:T(2,128)(2,1)}), bf16[2,1,1024,1024]{3,0,1,2:T(2,128)(2,1)}, u32[]{:S(2)}, u32[]{:S(2)}) async-start(bf16[2,1,1024,1024]{3,0,1,2:T(2,128)(2,1)} %copy.195), calls=%async_computation.6 | async-start | bytes 8388608 | tf_op jit(solution)/shard_map/all_to_all | solution.py:195
  484.5 200.9 %copy-start.1 = (bf16[1,192,2048]{2,1,0:T(8,128)(2,1)S(1)}, bf16[1,192,2048]{2,1,0:T(8,128)(2,1)}, u32[]{:S(2)}) copy-start(bf16[1,192,2048]{2,1,0:T(8,128)(2,1)} %param.25) | copy-start | bytes 2359300
Sparse Core Ops, SparseCore 0:
  34.9 98.6 all-gather.5
  135.7 76.7 all-gather.7
  342.6 14.2 all-gather.9
where the time goes:
time: 700 us; the launch traced here: 692 us
  waiting for transfers between devices  317 us (45%)
  blocking collectives  190 us (27%)
  local copies, waits for them, and re-layouts  71.6 us (10%)
  other arithmetic  47.6 us (7%)
  starting transfers between devices  29.5 us (4%)
  matrix products  21.9 us (3%)
  between operations  14.3 us (2%)
    all_to_all x1, waiting for transfers between devices, body(): lax.all_to_all(swapped, EP, split_axis=2, concat_axis=1, tiled=True)  187 us
    all_to_all x1, blocking collectives, body(): lax.all_to_all(outgoing, EP, split_axis=0, concat_axis=1, tiled=True)  118 us
    all_gather x2, waiting for transfers between devices, stacked_from(): pieces = lax.all_gather(pieces, axes[k], axis=0, tiled=True)  113 us
    all_gather x2, blocking collectives, stacked_from(): pieces = lax.all_gather(pieces, axes[k], axis=0, tiled=True)  52 us
    unnamed x1, other arithmetic  26 us
    unnamed x28, local copies, waits for them, and re-layouts  23.3 us
    all_to_all x1, starting transfers between devices, body(): lax.all_to_all(swapped, EP, split_axis=2, concat_axis=1, tiled=True)  21.4 us
    broadcast_in_dim x1, local copies, waits for them, and re-layouts, body(): partial_out[None]  20.6 us
  transfers between devices with their start and end apart: 6, of which 6 were waited for; matrix products, arithmetic and copies ran while one was open for 4% of the time, Pallas kernels for 0%

commit v1 on v0

--- a/solution.py
+++ b/solution.py
@@ -188,7 +188,10 @@
     outgoing = jnp.broadcast_to(
         outgoing.reshape(EXPERTS, 1, CAP, half_width), (EXPERTS, GROUPS, CAP, half_width)
     ).reshape(PIECES, CAP, half_width)
-    arrived_share = lax.all_to_all(outgoing, EP, split_axis=0, concat_axis=1, tiled=True)
+    n_dev = lax.axis_size(EP)
+    parts = jnp.stack(jnp.split(outgoing, n_dev, axis=0), axis=0)
+    parts = lax.all_to_all(parts, EP, split_axis=0, concat_axis=0)
+    arrived_share = jnp.concatenate(parts, axis=1)
     arrived = lax.all_gather(arrived_share, "tp", axis=2, tiled=True)
     partial_out = expert_block(arrived, gate_weight, up_weight, down_weight)
     swapped = lax.all_to_all(partial_out[None], "tp", split_axis=3, concat_axis=0, tiled=True)

time: 700 us -> 701 us (level)
    unnamed x28 -> x155, local copies, waits for them, and re-layouts: 23.3 us -> 23.7 us
where the time goes in v1:
time: 701 us; the launch traced here: 693 us
  waiting for transfers between devices  317 us (45%)
  blocking collectives  190 us (27%)
  local copies, waits for them, and re-layouts  72 us (10%)
  other arithmetic  47.6 us (7%)
  starting transfers between devices  29.9 us (4%)
  matrix products  21.9 us (3%)
  between operations  15.3 us (2%)
    all_to_all x1, waiting for transfers between devices, body(): lax.all_to_all(swapped, EP, split_axis=2, concat_axis=1, tiled=True)  187 us
    all_to_all x1, blocking collectives, body(): parts = lax.all_to_all(parts, EP, split_axis=0, concat_axis=0)  118 us
    all_gather x2, waiting for transfers between devices, stacked_from(): pieces = lax.all_gather(pieces, axes[k], axis=0, tiled=True)  113 us
    all_gather x2, blocking collectives, stacked_from(): pieces = lax.all_gather(pieces, axes[k], axis=0, tiled=True)  52 us
    unnamed x1, other arithmetic  26 us
    unnamed x155, local copies, waits for them, and re-layouts  23.7 us
    all_to_all x1, starting transfers between devices, body(): lax.all_to_all(swapped, EP, split_axis=2, concat_axis=1, tiled=True)  21.4 us
    broadcast_in_dim x1, local copies, waits for them, and re-layouts, body(): partial_out[None]  20.6 us
  transfers between devices with their start and end apart: 6, of which 6 were waited for; matrix products, arithmetic and copies ran while one was open for 4% of the time, Pallas kernels for 0%

profile of v1, /device:TPU:320, one launch (start us, length us, event | category | flops | bytes accessed | tf_op | source)
XLA Modules:
  0.0 693.4 jit_solution(1726210611363446255)
XLA Ops:
  7.3 26.9 %all-gather = bf16[64,4,128]{2,1,0:T(4,128)(2,1)S(1)} all-gather(bf16[8,4,128]{2,1,0:T(4,128)(2,1)} %param.18), channel_id=2, replica_groups=mesh['grp'=2,'ep_0'=8,'ep_1'=16,'tp'=2] {'ep_0'}, dimensions={0}, use_global_device_ids=true | all-gather | bytes 73728 | tf_op jit(solution)/shard_map/all_gather | solution.py:67
  34.9 25.1 %all-gather.1 = bf16[8192,16]{0,1:T(8,128)(2,1)S(1)} all-gather(bf16[1024,16]{0,1:T(8,128)(2,1)} %param.19), channel_id=3, replica_groups=mesh['grp'=2,'ep_0'=8,'ep_1'=16,'tp'=2] {'ep_0'}, dimensions={0}, use_global_device_ids=true | all-gather | bytes 294912 | tf_op jit(solution)/shard_map/all_gather | solution.py:67
  63.2 3.8 all-to-all-start
  69.3 3.2 fusion.4
  72.6 3.7 all_to_all.52
  85.8 4.0 all-to-all-start.2
  97.3 36.3 %all-gather.6.cloned.1.call-done = bf16[128,8,4,128]{3,1,2,0:T(8,128)(2,1)} async-done(((bf16[8,8,4,128]{3,1,2,0:T(8,128)(2,1)}), bf16[128,8,4,128]{3,1,2,0:T(8,128)(2,1)}) %all-gather.6.cloned.1.call-update) | async-done | bytes 1048592 | tf_op jit(solution)/shard_map/all_gather | solution.py:67
  135.9 76.6 %all-gather.8.cloned.1.call-done = bf16[128,1024,16]{1,0,2:T(8,128)(2,1)} async-done(((bf16[8,1024,16]{1,0,2:T(8,128)(2,1)}), bf16[128,1024,16]{1,0,2:T(8,128)(2,1)}) %all-gather.8.cloned.1.call-update) | async-done | bytes 4194320 | tf_op jit(solution)/shard_map/all_gather | solution.py:67
  212.5 4.5 copy.188
  218.5 4.7 all_to_all.53
  225.9 117.7 %all_to_all.54 = bf16[128,1,8,1024]{3,2,1,0:T(8,128)(2,1)} all-to-all(bf16[128,1,8,1024]{3,2,1,0:T(8,128)(2,1)S(1)} %constant_dynamic-update-slice_fusion), channel_id=1, replica_groups=mesh['grp'=2,'ep_0'=8,'ep_1'=16,'tp'=2] {'ep_0','ep_1'}, dimensions={0} | all-to-all | bytes 4194304 | tf_op jit(solution)/shard_map/all_to_all | solution.py:193
  343.7 14.4 %all-gather.10.cloned.1.call-done = bf16[1,1024,2048]{2,1,0:T(8,128)(2,1)} async-done(((bf16[1,1024,1024]{2,1,0:T(8,128)(2,1)}), bf16[1,1024,2048]{2,1,0:T(8,128)(2,1)}) %all-gather.10.cloned.1.call-update) | async-done | bytes 4194320 | tf_op jit(solution)/shard_map/all_gather | solution.py:195
  358.1 4.6 fusion.2
  362.7 7.3 %convert_bitcast_fusion = bf16[1,1,1024,2048]{3,2,1,0:T(8,128)(2,1)} fusion(bf16[1,192,2048]{2,1,0:T(8,128)(2,1)S(1)} %copy-done, bf16[1,1024,2048]{2,1,0:T(8,128)(2,1)} %all-gather.10.cloned.1.call-done, bf16[1,2048,192]{1,2,0:T(8,128)(2,1)} %param.24, f32[1024,192]{0,1:T(8,128)} %fusion.2), kind=kOutput, calls=%fused_computation.6 | convolution fusion | flops 1613889536 | bytes 10747904 | tf_op jit(solution)/shard_map/prf,pfd->prd/dot_general | solution.py:112
  370.0 20.6 %copy.194 = bf16[1,1,1024,2048]{2,1,0,3:T(2,128)(2,1)} copy(bf16[1,1,1024,2048]{3,2,1,0:T(8,128)(2,1)} %convert_bitcast_fusion) | data formatting | bytes 8388608 | tf_op jit(solution)/shard_map/broadcast_in_dim | solution.py:197
  391.1 26.0 %reduce.4 = bf16[2048,1024]{1,0:T(8,128)(2,1)} reduce(bf16[2048,1,1,1024]{3,2,1,0:T(2,128)(2,1)} %bitcast.614, bf16[]{:T(256)} %broadcast.147), dimensions={1,2}, to_apply=%bitcast.597.reduce_sub_computation | reduce | bytes 8388610
  417.0 5.9 reshape.242
  422.9 11.9 %all_to_all.55 = bf16[2,2,524288]{2,1,0:T(2,128)(2,1)} all-to-all(bf16[2,2,524288]{2,1,0:T(2,128)(2,1)} %reshape.242), channel_id=1, replica_groups=mesh['grp'=2,'ep_0'=8,'ep_1'=16,'tp'=2] {'tp'}, dimensions={0} | all-to-all | bytes 8388608 | tf_op jit(solution)/shard_map/all_to_all | solution.py:197
  434.9 7.1 %reshape.243 = bf16[2048,1,1,1024]{3,2,1,0:T(2,128)(2,1)} reshape(bf16[2,2,524288]{2,1,0:T(2,128)(2,1)} %all_to_all.55) | data formatting | bytes 8388608
  441.9 7.1 %copy.200 = bf16[1,1,1024,2048]{2,3,0,1:T(8,128)(2,1)} copy(bf16[1,1,1024,2048]{2,1,0,3:T(2,128)(2,1)} %bitcast.615) | data formatting | bytes 8388608
  449.0 11.3 %copy.195 = bf16[2,1,1024,1024]{3,0,1,2:T(2,128)(2,1)} copy(bf16[2,1,1024,1024]{2,3,0,1:T(8,128)(2,1)} %bitcast.616) | data formatting | bytes 8388608 | tf_op jit(solution)/shard_map/all_to_all | solution.py:197
  460.3 21.4 %all-to-all-start.6 = ((bf16[2,1,1024,1024]{3,0,1,2:T(2,128)(2,1)}), bf16[2,1,1024,1024]{3,0,1,2:T(2,128)(2,1)}, u32[]{:S(2)}, u32[]{:S(2)}) async-start(bf16[2,1,1024,1024]{3,0,1,2:T(2,128)(2,1)} %copy.195), calls=%async_computation.6 | async-start | bytes 8388608 | tf_op jit(solution)/shard_map/all_to_all | solution.py:198
  486.4 186.6 %all-to-all-done.6 = bf16[2,1,1024,1024]{3,0,1,2:T(2,128)(2,1)} async-done(((bf16[2,1,1024,1024]{3,0,1,2:T(2,128)(2,1)}), bf16[2,1,1024,1024]{3,0,1,2:T(2,128)(2,1)}, u32[]{:S(2)}, u32[]{:S(2)}) %all-to-all-start.6) | async-done | bytes 4194336 | tf_op jit(solution)/shard_map/all_to_all | solution.py:198
  673.0 12.4 %convert_reduce_fusion = bf16[1024,1024]{1,0:T(8,128)(2,1)S(1)} fusion(bf16[2,1,1024,1024]{3,0,1,2:T(2,128)(2,1)} %all-to-all-done.6), kind=kLoop, calls=%fused_computation.1 | loop fusion | flops 3145728 | bytes 6291456 | tf_op jit(solution)/shard_map/tk,qkd->td/reduce_sum | solution.py:200
  (210 shorter events, 35.1 us)
Async XLA Ops:
  7.2 355.5 %copy-start = (bf16[1,192,2048]{2,1,0:T(8,128)(2,1)S(1)}, bf16[1,192,2048]{2,1,0:T(8,128)(2,1)}, u32[]{:S(2)}) copy-start(bf16[1,192,2048]{2,1,0:T(8,128)(2,1)} %param.25) | copy-start | bytes 2359300
  7.2 126.4 %all-gather.6.cloned.1.call-start = ((), (), s32[]{:S(2)}) async-start(), calls=%async_computation.7 | async-start | bytes 1114112 | tf_op jit(solution)/shard_map/all_gather | solution.py:67
  34.8 177.6 %all-gather.8.cloned.1.call-start = ((), (), s32[]{:S(2)}) async-start(), calls=%async_computation.8 | async-start | bytes 4456448 | tf_op jit(solution)/shard_map/all_gather | solution.py:67
  63.2 5.4 copy-start.6
  63.2 5.4 copy-start.7
  63.2 6.1 all-to-all-start
  85.8 4.6 copy-start.4
  85.8 7.2 %all-to-all-start.2 = ((f32[2,64,8,513]{3,2,1,0:T(8,128)}), f32[2,64,8,513]{3,2,1,0:T(8,128)S(1)}, u32[]{:S(2)}, u32[]{:S(2)}) async-start(f32[2,64,8,513]{3,2,1,0:T(8,128)} %maximum_bitcast_fusion), calls=%async_computation.2 | async-start | bytes 5242880 | tf_op jit(solution)/shard_map/all_to_all | solution.py:49
  89.8 268.3 %all-gather.10.cloned.1.call-start = ((), (), s32[]{:S(2)}) async-start(), calls=%async_computation.9 | async-start | bytes 6291456 | tf_op jit(solution)/shard_map/all_gather | solution.py:195
  218.5 4.9 copy-start.3
  218.5 5.0 copy-start.5
  343.6 14.5 %copy-start.8 = (bf16[1,2048,192]{1,2,0:T(8,128)(2,1)S(1)}, bf16[1,2048,192]{1,2,0:T(8,128)(2,1)}, u32[]{:S(2)}) copy-start(bf16[1,2048,192]{1,2,0:T(8,128)(2,1)} %param.23) | copy-start | bytes 2359300
  460.3 21.7 %copy-start.2 = (bf16[2048,64]{0,1:T(8,128)(2,1)S(1)}, bf16[2048,64]{0,1:T(8,128)(2,1)}, u32[]{:S(2)}) copy-start(bf16[2048,64]{0,1:T(8,128)(2,1)} %param.21) | copy-start | bytes 786436
  460.3 212.7 %all-to-all-start.6 = ((bf16[2,1,1024,1024]{3,0,1,2:T(2,128)(2,1)}), bf16[2,1,1024,1024]{3,0,1,2:T(2,128)(2,1)}, u32[]{:S(2)}, u32[]{:S(2)}) async-start(bf16[2,1,1024,1024]{3,0,1,2:T(2,128)(2,1)} %copy.195), calls=%async_computation.6 | async-start | bytes 8388608 | tf_op jit(solution)/shard_map/all_to_all | solution.py:198
  673.0 13.6 %copy-start.1 = (bf16[1,192,2048]{2,1,0:T(8,128)(2,1)S(1)}, bf16[1,192,2048]{2,1,0:T(8,128)(2,1)}, u32[]{:S(2)}) copy-start(bf16[1,192,2048]{2,1,0:T(8,128)(2,1)} %param.25) | copy-start | bytes 2359300
Sparse Core Ops, SparseCore 0:
  34.9 98.6 all-gather.5
  135.7 76.6 all-gather.7
  343.8 14.2 all-gather.9
